TPU v7x, 32 devices: a whole 2x2x4 slice. The times are simulated.
32 devices in a mesh: gx: 8 (over y, x, core), gy: 4 (over z).
Axes of the slice: x: 2, y: 2, z: 4, core: 2. Of those that a mesh axis runs over, the one named last changes fastest.
Arguments:
- positions: float32 [3, 8, 4, 128], P(None, 'gx', 'gy'), may hold values from 0 to 384, as said below
- neighbours: int32 [32, 8, 4, 128], P(None, 'gx', 'gy'), may hold values from 0 to 1151, as said below
- live_count: int32 [8, 4], P('gx', 'gy'), may hold values from 16 to 128, as said below
- stencil_base: int32 [3, 8, 4, 128], P(None, 'gx', 'gy'), may hold values from -1 to 383, as said below
- spline_weight: float32 [3, 4, 8, 4, 128], P(None, None, 'gx', 'gy'), may hold values from 0 to 1, as said below
- spline_slope: float32 [3, 4, 8, 4, 128], P(None, None, 'gx', 'gy'), may hold values from -1 to 1, as said below
- embed_scale: float32 [100], replicated, may hold values from -12 to 12
- embed_bias: float32 [100], replicated, may hold values from -4 to 4
- desc_gain: float32 [1600], replicated, may hold values from 0.25 to 1.75
- fit_in: bfloat16 [128, 1600], replicated, may hold values from -0.15625 to 0.15625
- fit_bias: float32 [128], replicated, may hold values from -3 to 3
- fit_hidden: bfloat16 [128, 128], replicated, may hold values from -0.5 to 0.5
- fit_bias_two: float32 [128], replicated, may hold values from -3 to 3
- fit_out: float32 [128], replicated, may hold values from -0.5 to 0.5
Outputs:
- centroid_energy: float32 [8, 4, 128], P('gx', 'gy')
- centroid_force: float32 [3, 8, 4, 128], P(None, 'gx', 'gy')
Inputs may be any that keep to these rules, and one draw needn't show every extreme that they name: `live_count`: slots below a column's count are live; some column has all 128 slots live. `neighbours`: every entry names a live slot of one of the nine blocks of the column's neighbourhood. `stencil_base`: along x the base lies in -1 to 46, along y in -1 to 94, along z in 0 to 383. `positions`: x lies in 0 to 48, y in 0 to 96, z in 0 to 384. `spline_weight`: cubic B-spline weights of a fraction in [0, 1) for each axis; the four weights sum to one. `spline_slope`: the derivatives of those weights with respect to the fraction.
All inputs are finite; a program needn't handle non-finite values.
Results may differ from a plain program's by a relative error of at most 0.006.
The roundings to bfloat16 on the way count: a program that leaves them out, or rounds other values in their place, can miss the bound.
Values sent between devices are 32-bit elements; how exact they have to be, the bound alone decides.
A program may use at most 128 MiB of HBM per device.

v0:
```python
import math

import jax
import jax.numpy as jnp
from jax import lax
from jax.experimental import pallas as pl
from jax.experimental.pallas import tpu as pltpu
from jax.sharding import PartitionSpec as P

GRID = 384
AXIS = 16
LANES = 128
CHUNK = 512
TILE = 256

highest = lax.Precision.HIGHEST
radius_scale = 4.0
screen_width = 0.25
norm_floor = 1e-06
full_turn = 2.0 * math.pi


def charge_kernel(nearby_ref, listed_ref, scale_ref, bias_ref, mixed_ref, env_ref):
    neigh, atoms = listed_ref.shape
    listed = listed_ref[...]
    slot = listed % atoms
    block = listed // atoms
    square = jnp.zeros((neigh, atoms), jnp.float32)
    deltas = []
    for c in range(3):
        center = nearby_ref[c, 4:5, :]
        picked = jnp.zeros((neigh, atoms), jnp.float32)
        for b in range(9):
            row = jnp.broadcast_to(nearby_ref[c, b : b + 1, :], (neigh, atoms))
            got = jnp.take_along_axis(row, slot, axis=1, mode="promise_in_bounds")
            picked = jnp.where(block == b, got, picked)
        delta = picked - center
        deltas.append(delta)
        square = square + delta * delta
    radius = jnp.sqrt(square)
    smooth = 1.0 / (1.0 + radius / radius_scale)
    factor = smooth / (radius + radius_scale)
    env_ref[0] = smooth
    for c in range(3):
        env_ref[c + 1] = deltas[c] * factor
    mixed_ref[...] = jnp.zeros_like(mixed_ref)

    def step(k, carry):
        row = env_ref[0, pl.ds(k, 1), :]
        embed = jnp.tanh(row * scale_ref[...] + bias_ref[...])
        for c in range(4):
            mixed_ref[c] += embed * env_ref[c, pl.ds(k, 1), :]
        return carry

    lax.fori_loop(0, neigh, step, 0)


def mixed_features(nearby, listed, embed_scale, embed_bias):
    neigh, atoms = listed.shape
    width = embed_scale.shape[0]
    spread = jnp.broadcast_to(embed_scale[:, None], (width, atoms))
    shift = jnp.broadcast_to(embed_bias[:, None], (width, atoms))
    return pl.pallas_call(
        charge_kernel,
        out_shape=jax.ShapeDtypeStruct((4, width, atoms), jnp.float32),
        scratch_shapes=[pltpu.VMEM((4, neigh, atoms), jnp.float32)],
    )(nearby, listed, spread, shift)


def fit_charge(mixed, count, desc_gain, fit_in, fit_bias, fit_hidden, fit_bias_two, fit_out):
    atoms = mixed.shape[2]
    descriptor = jnp.sum(mixed[:, :, None, :] * mixed[:, None, :AXIS, :], axis=0).reshape(-1, atoms)
    scaling = lax.rsqrt(jnp.mean(descriptor * descriptor, axis=0) + norm_floor)
    normed = (descriptor * scaling[None, :] * desc_gain[:, None]).astype(jnp.bfloat16)
    first = jnp.tanh(
        jnp.dot(fit_in, normed, preferred_element_type=jnp.float32) + fit_bias[:, None]
    )
    second = (
        jnp.tanh(
            jnp.dot(fit_hidden, first.astype(jnp.bfloat16), preferred_element_type=jnp.float32)
            + fit_bias_two[:, None]
        )
        + first
    )
    charge = jnp.sum(fit_out[:, None] * second, axis=0)
    slot_index = lax.broadcasted_iota(jnp.int32, (atoms,), 0)
    return jnp.where(slot_index < count, charge, jnp.zeros((), charge.dtype))


def pack_kernel(count_ref, sites_ref, packed_ref):
    columns, rows, atoms = sites_ref.shape
    packed_ref[...] = jnp.zeros_like(packed_ref)
    lane = lax.broadcasted_iota(jnp.int32, (rows, atoms), 1)

    def step(j, start):
        count = count_ref[j]
        tile = start // atoms
        shift = start % atoms
        block = jnp.where(lane < count, sites_ref[j], 0.0)
        turned = pltpu.roll(block, shift, 1)
        packed_ref[tile] = packed_ref[tile] + jnp.where(lane >= shift, turned, 0.0)
        packed_ref[tile + 1] = jnp.where(lane < shift, turned, 0.0)
        return start + count

    lax.fori_loop(0, columns, step, 0)


def pack_sites(counts, sites):
    columns, rows, atoms = sites.shape
    return pl.pallas_call(
        pack_kernel,
        in_specs=[
            pl.BlockSpec(memory_space=pltpu.SMEM),
            pl.BlockSpec(memory_space=pltpu.VMEM),
        ],
        out_specs=pl.BlockSpec(memory_space=pltpu.VMEM),
        out_shape=jax.ShapeDtypeStruct((columns + 1, rows, atoms), jnp.float32),
    )(counts, sites)


def axis_waves(cell, start, groups):
    def turn(index):
        angle = ((index * cell[None, :]) % GRID).astype(jnp.float32) * (full_turn / GRID)
        return jnp.cos(angle), jnp.sin(angle)

    low_cos, low_sin = turn(jnp.arange(8, dtype=jnp.int32)[:, None])
    high_cos, high_sin = turn(start + 8 * jnp.arange(groups, dtype=jnp.int32)[:, None])
    low_cos, low_sin = low_cos[None], low_sin[None]
    high_cos, high_sin = high_cos[:, None], high_sin[:, None]
    cosine = high_cos * low_cos - high_sin * low_sin
    sine = high_sin * low_cos + high_cos * low_sin
    return cosine.reshape(groups * 8, -1), sine.reshape(groups * 8, -1)


def axis_table(cosine, sine, taps, start):
    count = cosine.shape[0]
    angle = (start + jnp.arange(count, dtype=jnp.int32)).astype(jnp.float32) * (full_turn / GRID)
    angle = angle[:, None]
    real = taps[1] + (taps[0] + taps[2]) * jnp.cos(angle) + taps[3] * jnp.cos(2.0 * angle)
    imag = (taps[2] - taps[0]) * jnp.sin(angle) + taps[3] * jnp.sin(2.0 * angle)
    return cosine * real - sine * imag, sine * real + cosine * imag


def plane_tables(cell, taps, slopes, start, groups):
    cosine, sine = axis_waves(cell, start, groups)
    parity = (1 - 2 * (cell % 2)).astype(jnp.float32)
    zero_mode = (start + jnp.arange(groups * 8, dtype=jnp.int32) == 0)[:, None]
    tables = []
    for row in (taps, slopes):
        even, odd = axis_table(cosine, sine, row, start)
        last = parity * (row[1] + row[3] - row[0] - row[2])
        tables.append(jnp.concatenate([even, jnp.where(zero_mode, last[None], odd)], axis=0))
    return tables


def plane_modes(start, count):
    mode = start + jnp.arange(count, dtype=jnp.int32)
    modes = jnp.concatenate([mode, jnp.where(mode == 0, GRID // 2, mode)])
    factor = jnp.where((modes == 0) | (modes == GRID // 2), 1.0, 2.0) / GRID
    wave = modes.astype(jnp.float32) * (full_turn / GRID)
    return wave * wave, factor.astype(jnp.float32)


def halves(table):
    high = lax.reduce_precision(table, 8, 7)
    low = table - high
    return jnp.concatenate([high, low], axis=0).astype(jnp.bfloat16)


def mesh_kernel(
    count_ref,
    squares_ref,
    factors_ref,
    square_y_ref,
    square_z_ref,
    charge_ref,
    x_ref,
    slope_x_ref,
    y_ref,
    slope_y_ref,
    z_ref,
    slope_z_ref,
    out_ref,
    spectrum_ref,
    scaled_ref,
    found_ref,
):
    modes_x = x_ref.shape[0]
    modes_y = y_ref.shape[0]
    depth = z_ref.shape[0]
    modes_z = depth // 2
    columns = out_ref.shape[0]
    group = 8
    total = lax.fori_loop(0, columns, lambda j, acc: acc + count_ref[j], 0)
    spectrum_ref[...] = jnp.zeros_like(spectrum_ref)

    def gather_chunk(chunk, carry):
        lanes = pl.ds(pl.multiple_of(chunk * CHUNK, CHUNK), CHUNK)
        y = y_ref[:, lanes] * charge_ref[:, lanes]
        high = z_ref[:modes_z, lanes]
        low = z_ref[modes_z:, lanes]

        def rows(g, inner):
            x = x_ref[pl.ds(pl.multiple_of(g * group, group), group), lanes]
            left = jnp.concatenate(
                [(x[a : a + 1] * y).astype(jnp.bfloat16) for a in range(group)], axis=0
            )
            where = pl.ds(pl.multiple_of(g * group * modes_y, group * modes_y), group * modes_y)
            form = (((1,), (1,)), ((), ()))
            spectrum_ref[where, :] += lax.dot_general(
                left, high, form, preferred_element_type=jnp.float32
            ) + lax.dot_general(left, low, form, preferred_element_type=jnp.float32)
            return inner

        return lax.fori_loop(0, modes_x // group, rows, carry)

    lax.fori_loop(0, (total + CHUNK - 1) // CHUNK, gather_chunk, 0)

    square_y = square_y_ref[:, 0:1]
    factor_y = square_y_ref[:, 1:2]
    square_z = square_z_ref[0:1, :]
    factor_z = square_z_ref[1:2, :]
    plane = square_y + square_z
    weight = factor_y * factor_z * (2.0 * full_turn)

    def scale(a, carry):
        square = plane + squares_ref[a]
        safe = jnp.where(square > 0, square, 1.0)
        green = jnp.exp(square * (-0.5 * screen_width * screen_width)) / safe
        green = jnp.where(square > 0, green, 0.0) * (weight * factors_ref[a])
        where = pl.ds(pl.multiple_of(a * modes_y, modes_y), modes_y)
        value = (spectrum_ref[where, :] * green).astype(jnp.bfloat16)
        scaled_ref[where, :modes_z] = value
        scaled_ref[where, modes_z:] = value
        return carry

    lax.fori_loop(0, modes_x, scale, 0)
    found_ref[...] = jnp.zeros_like(found_ref)

    def tile_step(tile, carry):
        lanes = pl.ds(pl.multiple_of(tile * TILE, TILE), TILE)
        y = y_ref[:, lanes]
        slope_y = slope_y_ref[:, lanes]
        z = z_ref[:, lanes]
        slope_z = slope_z_ref[:, lanes]

        def rows(g, sums):
            spot = pl.ds(pl.multiple_of(g * group, group), group)
            x = x_ref[spot, lanes]
            slope_x = slope_x_ref[spot, lanes]
            where = pl.ds(pl.multiple_of(g * group * modes_y, group * modes_y), group * modes_y)
            left = scaled_ref[where, :]
            along = jnp.dot(left, z, preferred_element_type=jnp.float32)
            slant = jnp.dot(left, slope_z, preferred_element_type=jnp.float32)
            value, field_x, field_y, field_z = sums
            for a in range(group):
                part = along[a * modes_y : (a + 1) * modes_y]
                skew = slant[a * modes_y : (a + 1) * modes_y]
                over = jnp.sum((part * y).reshape(modes_y // 8, 8, TILE), axis=0)
                tilt = jnp.sum((part * slope_y).reshape(modes_y // 8, 8, TILE), axis=0)
                deep = jnp.sum((skew * y).reshape(modes_y // 8, 8, TILE), axis=0)
                row = x[a : a + 1]
                value = value + over * row
                field_x = field_x + over * slope_x[a : a + 1]
                field_y = field_y + tilt * row
                field_z = field_z + deep * row
            return value, field_x, field_y, field_z

        zero = jnp.zeros((8, TILE), jnp.float32)
        sums = lax.fori_loop(0, modes_x // group, rows, (zero, zero, zero, zero))
        for part in range(TILE // LANES):
            for c in range(4):
                found_ref[tile * (TILE // LANES) + part, c : c + 1, :] = jnp.sum(
                    sums[c][:, part * LANES : (part + 1) * LANES], axis=0, keepdims=True
                )
        return carry

    lax.fori_loop(0, (total + TILE - 1) // TILE, tile_step, 0)
    lane = lax.broadcasted_iota(jnp.int32, (8, LANES), 1)

    def place(j, start):
        tile = start // LANES
        shift = start % LANES
        back = (LANES - shift) % LANES
        first = pltpu.roll(found_ref[tile], back, 1)
        second = pltpu.roll(found_ref[tile + 1], back, 1)
        out_ref[j] = jnp.where(lane < LANES - shift, first, second)
        return start + count_ref[j]

    lax.fori_loop(0, columns, place, 0)


def mesh_sums(counts, squares_x, factors_x, side_y, side_z, charge, tables):
    columns = counts.shape[0]
    modes_x = tables[0].shape[0]
    modes_y = tables[2].shape[0]
    modes_z = tables[4].shape[0] // 2
    vmem = pl.BlockSpec(memory_space=pltpu.VMEM)
    smem = pl.BlockSpec(memory_space=pltpu.SMEM)
    return pl.pallas_call(
        mesh_kernel,
        in_specs=[smem, smem, smem] + [vmem] * 9,
        out_specs=vmem,
        out_shape=jax.ShapeDtypeStruct((columns, 8, LANES), jnp.float32),
        scratch_shapes=[
            pltpu.VMEM((modes_x * modes_y, modes_z), jnp.float32),
            pltpu.VMEM((modes_x * modes_y, 2 * modes_z), jnp.bfloat16),
            pltpu.VMEM((tables[0].shape[1] // LANES + 2, 8, LANES), jnp.float32),
        ],
        compiler_params=pltpu.CompilerParams(vmem_limit_bytes=60 * 2**20),
    )(counts, squares_x, factors_x, side_y, side_z, charge, *tables)


def local_sites(
    positions,
    neighbours,
    live_count,
    stencil_base,
    spline_weight,
    spline_slope,
    embed_scale,
    embed_bias,
    desc_gain,
    fit_in,
    fit_bias,
    fit_hidden,
    fit_bias_two,
    fit_out,
):
    both = ("gx", "gy")
    columns_x = lax.axis_size("gx")
    columns_y = lax.axis_size("gy")
    columns = columns_x * columns_y
    place_x = lax.axis_index("gx")
    place_y = lax.axis_index("gy")
    width_x = GRID // columns_x
    width_y = GRID // columns_y
    atoms = positions.shape[3]
    origin = jnp.stack([place_x * width_x, place_y * width_y, 0])
    cells = (stencil_base[:, 0, 0, :] + origin[:, None] + 1).astype(jnp.float32)
    counted = jnp.broadcast_to(live_count.astype(jnp.float32), (1, atoms))
    parcel = jnp.concatenate(
        [
            positions[:, 0, 0, :],
            counted,
            cells,
            spline_weight[:, :, 0, 0, :].reshape(12, atoms),
            spline_slope[:, :, 0, 0, :].reshape(12, atoms),
        ],
        axis=0,
    )
    shared = lax.all_gather(parcel, both, axis=0, tiled=False)
    counts = shared[:, 3, 0].astype(jnp.int32)
    near = []
    for stride_x in (-1, 0, 1):
        for stride_y in (-1, 0, 1):
            other_x = (place_x + stride_x) % columns_x
            other_y = (place_y + stride_y) % columns_y
            block = lax.dynamic_index_in_dim(
                shared, other_x * columns_y + other_y, axis=0, keepdims=False
            )[:3]
            offset = jnp.array([stride_x * width_x, stride_y * width_y, 0], jnp.float32)
            near.append(block + offset[:, None])
    mixed = mixed_features(
        jnp.stack(near, axis=1), neighbours[:, 0, 0, :], embed_scale, embed_bias
    )
    charge = fit_charge(
        mixed, live_count[0, 0], desc_gain, fit_in, fit_bias, fit_hidden, fit_bias_two, fit_out
    )
    charges = lax.all_gather(charge, both, axis=0, tiled=False)
    sites = jnp.concatenate(
        [shared[:, 4:], charges[:, None, :], jnp.zeros((columns, 4, atoms), jnp.float32)], axis=1
    )
    packed = pack_sites(counts, sites)[:columns]
    slots = -(-(columns * atoms) // CHUNK) * CHUNK
    packed = jnp.transpose(packed, (1, 0, 2)).reshape(packed.shape[1], columns * atoms)
    packed = jnp.pad(packed, ((0, 0), (0, slots - columns * atoms)))
    cells = packed[:3].astype(jnp.int32)
    taps = packed[3:15].reshape(3, 4, -1)
    slopes = packed[15:27].reshape(3, 4, -1)
    half_x = GRID // columns_x // 2
    half_y = GRID // columns_y // 2
    start_x = place_x * half_x
    start_y = place_y * half_y
    table_x, slope_x = plane_tables(cells[0], taps[0], slopes[0], start_x, half_x // 8)
    table_y, slope_y = plane_tables(cells[1], taps[1], slopes[1], start_y, half_y // 8)
    cosine, sine = axis_waves(cells[2], 0, GRID // 16)
    table_z = halves(jnp.concatenate(axis_table(cosine, sine, taps[2], 0), axis=0))
    slope_z = halves(jnp.concatenate(axis_table(cosine, sine, slopes[2], 0), axis=0))
    squares_x, factors_x = plane_modes(start_x, half_x)
    squares_y, factors_y = plane_modes(start_y, half_y)
    mode_z = jnp.arange(GRID, dtype=jnp.int32) % (GRID // 2)
    wave_z = mode_z.astype(jnp.float32) * (full_turn / GRID)
    factors_z = jnp.where(mode_z == 0, 1.0, 2.0).astype(jnp.float32) / GRID
    side_y = jnp.stack([squares_y, factors_y], axis=1)
    side_z = jnp.stack([wave_z * wave_z, factors_z], axis=0)
    sums = mesh_sums(
        counts,
        squares_x,
        factors_x,
        side_y,
        side_z,
        packed[27:28],
        (table_x, slope_x, table_y, slope_y, table_z, slope_z),
    )
    mine = lax.psum_scatter(sums[:, :4], both, scatter_dimension=0, tiled=True)[0]
    energy = (0.5 * charge * mine[0]).reshape(1, 1, atoms)
    force = (-charge[None, :] * mine[1:]).reshape(3, 1, 1, atoms)
    return (energy, force)


def padded_2(shard, sides, width):
    for axis, dim in sides:
        peers, length = (lax.axis_size(axis), shard.shape[dim])
        up = [(i, (i + 1) % peers) for i in range(peers)]
        down = [(j, i) for i, j in up]
        last = lax.slice_in_dim(shard, length - width, length, axis=dim)
        leading = lax.slice_in_dim(shard, 0, width, axis=dim)
        before = lax.ppermute(last, axis, up)
        after = lax.ppermute(leading, axis, down)
        shard = jnp.concatenate([before, shard, after], axis=dim)
    return shard


def shifted(block, axis, distance):
    devices = range(lax.axis_size(axis))
    route = [((i - distance) % len(devices), i) for i in devices]
    return lax.ppermute(block, axis, route)


def stencil_table(anchor, weights, length, offset, periodic):
    count = anchor.shape[0]
    cell_index = lax.broadcasted_iota(jnp.int32, (4, length, count), 1)
    tap_index = lax.broadcasted_iota(jnp.int32, (4, length, count), 0)
    target = anchor[None, None, :] + tap_index + offset
    if periodic:
        target = target % length
    chosen = jnp.where(target == cell_index, weights[:, None, :], jnp.zeros((), weights.dtype))
    return jnp.sum(chosen, axis=0)


def spread_cells(charge, anchor, weights, extent_x, extent_y, offset, length):
    table_x = stencil_table(anchor[0], weights[0] * charge[None, :], extent_x, offset, False)
    table_y = stencil_table(anchor[1], weights[1], extent_y, offset, False)
    table_z = stencil_table(anchor[2], weights[2], length, 0, True)
    planes = (table_x[:, None, :] * table_y[None, :, :]).reshape(extent_x * extent_y, -1)
    return jnp.dot(planes, table_z.T, precision=highest).reshape(extent_x, extent_y, length)


def interpolate(padded, anchor, weights, slopes):
    extent_x, extent_y, length = padded.shape
    table_x = stencil_table(anchor[0], weights[0], extent_x, 2, False)
    slope_x = stencil_table(anchor[0], slopes[0], extent_x, 2, False)
    table_y = stencil_table(anchor[1], weights[1], extent_y, 2, False)
    slope_y = stencil_table(anchor[1], slopes[1], extent_y, 2, False)
    table_z = stencil_table(anchor[2], weights[2], length, 0, True)
    slope_z = stencil_table(anchor[2], slopes[2], length, 0, True)
    flat = padded.reshape(extent_x * extent_y, length)
    along = jnp.dot(flat, table_z, precision=highest).reshape(extent_x, extent_y, -1)
    slant = jnp.dot(flat, slope_z, precision=highest).reshape(extent_x, extent_y, -1)
    over_y = jnp.sum(along * table_y[None], axis=1)
    value = jnp.sum(table_x * over_y, axis=0)
    field_x = -jnp.sum(slope_x * over_y, axis=0)
    over_x = jnp.sum(along * table_x[:, None, :], axis=0)
    field_y = -jnp.sum(slope_y * over_x, axis=0)
    slant_y = jnp.sum(slant * table_y[None], axis=1)
    field_z = -jnp.sum(table_x * slant_y, axis=0)
    return (value, jnp.stack([field_x, field_y, field_z]))


def fitted_charge(
    nearby,
    listed,
    count,
    embed_scale,
    embed_bias,
    desc_gain,
    fit_in,
    fit_bias,
    fit_hidden,
    fit_bias_two,
    fit_out,
):
    atoms = listed.shape[1]
    center = nearby[:, 4 * atoms : 5 * atoms]
    picked = jnp.take(nearby, listed.reshape(-1), axis=1).reshape(3, listed.shape[0], atoms)
    delta = picked - center[:, None, :]
    radius = jnp.sqrt(jnp.sum(delta * delta, axis=0))
    smooth = 1.0 / (1.0 + radius / radius_scale)
    factor = smooth / (radius + radius_scale)
    envelope = jnp.concatenate([smooth[None], delta * factor[None]], axis=0)
    embed = jnp.tanh(smooth[None] * embed_scale[:, None, None] + embed_bias[:, None, None])
    mixed = jnp.einsum("ekn,ckn->ecn", embed, envelope, precision=highest)
    descriptor = jnp.einsum("ecn,acn->ean", mixed, mixed[:AXIS], precision=highest).reshape(
        -1, atoms
    )
    scaling = lax.rsqrt(jnp.mean(descriptor * descriptor, axis=0) + norm_floor)
    normed = (descriptor * scaling[None, :] * desc_gain[:, None]).astype(jnp.bfloat16)
    first = jnp.tanh(
        jnp.dot(fit_in, normed, preferred_element_type=jnp.float32) + fit_bias[:, None]
    )
    second = (
        jnp.tanh(
            jnp.dot(fit_hidden, first.astype(jnp.bfloat16), preferred_element_type=jnp.float32)
            + fit_bias_two[:, None]
        )
        + first
    )
    charge = jnp.sum(fit_out[:, None] * second, axis=0)
    slot_index = lax.broadcasted_iota(jnp.int32, (atoms,), 0)
    return jnp.where(slot_index < count, charge, jnp.zeros((), charge.dtype))


def wave_number(index, length):
    signed = jnp.where(index > length // 2, index - length, index)
    return signed.astype(jnp.float32) * (full_turn / length)


def green_values(index_x, index_y, index_z, length):
    wave_x = wave_number(index_x, length)
    wave_y = wave_number(index_y, length)
    wave_z = wave_number(index_z, length)
    square = wave_x * wave_x + wave_y * wave_y + wave_z * wave_z
    safe = jnp.where(square > 0, square, 1.0)
    value = 2.0 * full_turn * jnp.exp(-0.5 * screen_width * screen_width * square) / safe
    keep = (square > 0) & (index_z != length // 2)
    return jnp.where(keep, value, 0.0)


def wave_tables(length, count):
    rows = lax.broadcasted_iota(jnp.int32, (length, count), 0)
    cols = lax.broadcasted_iota(jnp.int32, (length, count), 1)
    angle = (rows * cols % length).astype(jnp.float32) * (full_turn / length)
    return (jnp.cos(angle), jnp.sin(angle))


def along_axis(real_part, imag_part, cosine, sine, sign, form):
    real_cos = jnp.einsum(form, real_part, cosine, precision=highest)
    real_sin = jnp.einsum(form, real_part, sine, precision=highest)
    imag_cos = jnp.einsum(form, imag_part, cosine, precision=highest)
    imag_sin = jnp.einsum(form, imag_part, sine, precision=highest)
    return (real_cos + sign * imag_sin, imag_cos - sign * real_sin)


def local_mesh(
    positions,
    neighbours,
    live_count,
    stencil_base,
    spline_weight,
    spline_slope,
    embed_scale,
    embed_bias,
    desc_gain,
    fit_in,
    fit_bias,
    fit_hidden,
    fit_bias_two,
    fit_out,
):
    columns_y = lax.axis_size("gy")
    width_x = GRID // lax.axis_size("gx")
    width_y = GRID // columns_y
    atoms = positions.shape[3]
    beside_all = padded_2(positions, (("gx", 1), ("gy", 2)), 1)
    block_x = lax.broadcasted_iota(jnp.int32, (3, 3, atoms), 0) - 1
    block_y = lax.broadcasted_iota(jnp.int32, (3, 3, atoms), 1) - 1
    offsets = jnp.stack([block_x * width_x, block_y * width_y, jnp.zeros_like(block_x)]).astype(
        jnp.float32
    )
    nearby = (beside_all + offsets).reshape(3, 9 * atoms)
    charge = fitted_charge(
        nearby,
        neighbours[:, 0, 0, :],
        live_count[0, 0],
        embed_scale,
        embed_bias,
        desc_gain,
        fit_in,
        fit_bias,
        fit_hidden,
        fit_bias_two,
        fit_out,
    )
    anchor = stencil_base[:, 0, 0, :]
    weights = spline_weight[:, :, 0, 0, :]
    slopes = spline_slope[:, :, 0, 0, :]
    spread = spread_cells(charge, anchor, weights, width_x + 4, width_y + 4, 2, GRID)
    inner = spread[2 : width_x + 2]
    for stride in (1, -1):
        piece = spread[width_x + 2 :] if stride == 1 else spread[:2]
        moved = shifted(piece, "gx", stride)
        if stride == 1:
            inner = inner.at[:2].add(moved)
        else:
            inner = inner.at[width_x - 2 :].add(moved)
    density = inner[:, 2 : width_y + 2]
    for stride in (1, -1):
        piece = inner[:, width_y + 2 :] if stride == 1 else inner[:, :2]
        moved = shifted(piece, "gy", stride)
        if stride == 1:
            density = density.at[:, :2].add(moved)
        else:
            density = density.at[:, width_y - 2 :].add(moved)
    freqs = GRID // 2
    fold_weight = jnp.where(jnp.arange(freqs) == 0, 1.0, 2.0).astype(jnp.float32) / GRID
    cosine_z, sine_z = wave_tables(GRID, freqs)
    flat = density.reshape(width_x * width_y, GRID)
    real_part = jnp.dot(flat, cosine_z, precision=highest).reshape(width_x, width_y, freqs)
    imag_part = -jnp.dot(flat, sine_z, precision=highest).reshape(width_x, width_y, freqs)
    real_part, imag_part = (
        lax.all_to_all(real_part, "gy", split_axis=2, concat_axis=1, tiled=True),
        lax.all_to_all(imag_part, "gy", split_axis=2, concat_axis=1, tiled=True),
    )
    cosine, sine = wave_tables(GRID, GRID)
    real_part, imag_part = along_axis(real_part, imag_part, cosine, sine, 1.0, "xym,yk->xkm")
    real_part, imag_part = (
        lax.all_to_all(real_part, "gx", split_axis=1, concat_axis=0, tiled=True),
        lax.all_to_all(imag_part, "gx", split_axis=1, concat_axis=0, tiled=True),
    )
    real_part, imag_part = along_axis(real_part, imag_part, cosine, sine, 1.0, "xym,xk->kym")
    span_y = real_part.shape[1]
    span_z = real_part.shape[2]
    index_x = lax.broadcasted_iota(jnp.int32, (GRID, span_y, span_z), 0)
    index_y = lax.axis_index("gx") * span_y + lax.broadcasted_iota(
        jnp.int32, (GRID, span_y, span_z), 1
    )
    index_z = lax.axis_index("gy") * span_z + lax.broadcasted_iota(
        jnp.int32, (GRID, span_y, span_z), 2
    )
    green = green_values(index_x, index_y, index_z, GRID)
    real_part = real_part * green
    imag_part = imag_part * green
    back_cos = cosine / GRID
    back_sin = sine / GRID
    real_part, imag_part = along_axis(real_part, imag_part, back_cos, back_sin, -1.0, "xym,xk->kym")
    real_part, imag_part = (
        lax.all_to_all(real_part, "gx", split_axis=0, concat_axis=1, tiled=True),
        lax.all_to_all(imag_part, "gx", split_axis=0, concat_axis=1, tiled=True),
    )
    real_part, imag_part = along_axis(real_part, imag_part, back_cos, back_sin, -1.0, "xym,yk->xkm")
    real_part, imag_part = (
        lax.all_to_all(real_part, "gy", split_axis=1, concat_axis=2, tiled=True),
        lax.all_to_all(imag_part, "gy", split_axis=1, concat_axis=2, tiled=True),
    )
    rows_y = real_part.shape[1]
    flat_real = real_part.reshape(width_x * rows_y, freqs)
    flat_imag = imag_part.reshape(width_x * rows_y, freqs)
    summed_cos = (cosine_z * fold_weight[None, :]).T
    summed_sin = (sine_z * fold_weight[None, :]).T
    potential = jnp.dot(flat_real, summed_cos, precision=highest) - jnp.dot(
        flat_imag, summed_sin, precision=highest
    )
    potential = potential.reshape(width_x, rows_y, GRID)
    padded = padded_2(potential, (("gx", 0), ("gy", 1)), 2)
    value, field = interpolate(padded, anchor, weights, slopes)
    energy = (0.5 * charge * value).reshape(1, 1, atoms)
    force = (charge[None, :] * field).reshape(3, 1, 1, atoms)
    return (energy, force)


def solution(mesh):
    def local(positions, *rest):
        columns_x, columns_y = (lax.axis_size("gx"), lax.axis_size("gy"))
        sites = columns_x * columns_y * positions.shape[3]
        whole = GRID % (16 * columns_x) == 0 and GRID % (16 * columns_y) == 0
        few = whole and sites <= 8 * GRID * 2
        return (local_sites if few and positions.shape[3] == LANES else local_mesh)(positions, *rest)

    placed = (
        P(None, "gx", "gy", None),
        P(None, "gx", "gy", None),
        P("gx", "gy"),
        P(None, "gx", "gy", None),
        P(None, None, "gx", "gy", None),
        P(None, None, "gx", "gy", None),
        P(),
        P(),
        P(),
        P(),
        P(),
        P(),
        P(),
        P(),
    )
    return jax.shard_map(
        local,
        mesh=mesh,
        in_specs=placed,
        out_specs=(P("gx", "gy", None), P(None, "gx", "gy", None)),
        check_vma=False,
    )
```

profile of v0, /device:TPU:0, one launch (start us, length us, event | category | flops | bytes accessed | tf_op | source)
XLA Modules:
  0.0 412.4 jit_solution(9175539223673196817)
XLA Ops:
  11.2 74.1 %all-gather.1 = f32[32,31,128]{2,1,0:T(8,128)S(1)} all-gather(f32[1,31,128]{2,1,0:T(8,128)S(1)} %bitcast.253), channel_id=2, replica_groups=mesh['gx'=8,'gy'=4] {'gx','gy'}, dimensions={0}, use_global_device_ids=true | all-gather | bytes 523776 | tf_op jit(solution)/shard_map/all_gather | solution.py:352
  85.3 1.2 fusion.76.count_ref
  89.5 1.2 stack.15.nearby_ref
  90.7 1.4 broadcast_in_dim.101.scale_ref
  92.1 1.4 broadcast_in_dim.104.bias_ref
  93.5 2.9 shard_map.230
  97.2 1.3 multiply_reduce_fusion
  99.6 63.4 %all-gather.2 = f32[32,1,128]{2,1,0:T(1,128)S(1)} all-gather(f32[1,1,128]{2,1,0:T(1,128)S(1)} %fusion.96), channel_id=1, replica_groups=mesh['gx'=8,'gy'=4] {'gx','gy'}, dimensions={0}, use_global_device_ids=true | all-gather | bytes 16896 | tf_op jit(solution)/shard_map/all_gather | solution.py:370
  163.1 0.9 maximum_maximum_fusion.sites_ref
  164.1 4.3 %shard_map.231 = f32[33,32,128]{2,1,0:T(8,128)} custom-call(s32[32]{0:T(128)} %fusion.76.count_ref, f32[32,32,128]{2,1,0:T(8,128)} %maximum_maximum_fusion.sites_ref), custom_call_target="tpu_custom_call" | custom-call | tf_op jit(solution)/shard_map/pallas_call | solution.py:110
  168.3 1.1 slice_bitcast_fusion
  170.4 0.8 bitcast_multiply_fusion.25
  171.2 0.9 fusion.111
  177.3 1.7 fusion.30
  178.9 1.2 fusion.47
  180.2 1.3 fusion.51
  181.5 1.2 fusion.55
  182.7 1.2 fusion.66
  184.8 3.7 fusion.4
  188.5 1.3 reduce-precision_convert_fusion
  189.8 3.5 pad_maximum_fusion.3.slope_z_ref
  193.3 1.2 reduce-precision_convert_fusion.1
  194.7 3.4 pad_maximum_fusion.1.z_ref
  198.2 1.5 bitcast_multiply_fusion.26
  199.9 0.9 fusion.13
  201.0 1.3 pad_maximum_fusion.5.slope_y_ref
  202.3 1.3 pad_maximum_fusion.4.y_ref
  204.2 0.9 pad_maximum_fusion.7.slope_x_ref
  205.2 1.0 pad_maximum_fusion.6.x_ref
  207.4 77.2 %shard_map.232 = f32[32,8,128]{2,1,0:T(8,128)} custom-call(s32[32]{0:T(128)} %fusion.76.count_ref, f32[48]{0:T(128)} %get-tuple-element.92.squares_ref, f32[48]{0:T(128)} %get-tuple-element.91.factors_ref, f32[96,2]{1,0:T(8,128)} %copy.53.square_y_ref, f32[2,384]{1,0:T(2,128)} %pad_maximum_fusion.8.square_z_ref, f32[1,4096]{1,0:T(1,128)} %get-tuple-element.56.charge_ref, ...), custom_call_target="tpu_custom_call" | custom-call | tf_op jit(solution)/shard_map/pallas_call | solution.py:300
  284.6 1.5 slice.372
  286.2 117.6 %all-reduce.3.cloned.1.call-done = f32[32,4,128]{2,1,0:T(4,128)} async-done(((f32[32,4,128]{2,1,0:T(4,128)}), f32[32,4,128]{2,1,0:T(4,128)}) %all-reduce.3.cloned.1.call-update) | async-done | bytes 65552
  (154 shorter events, 18.8 us)
Async XLA Ops:
  7.2 91.8 %copy-start = (bf16[128,1600]{0,1:T(8,128)(2,1)S(1)}, bf16[128,1600]{0,1:T(8,128)(2,1)}, u32[]{:S(2)}) copy-start(bf16[128,1600]{0,1:T(8,128)(2,1)} %param.32) | copy-start | bytes 1228804
  7.2 91.5 %copy-start.28 = (f32[1600]{0:T(1024)S(1)}, f32[1600]{0:T(1024)}, u32[]{:S(2)}) copy-start(f32[1600]{0:T(1024)} %param.31) | copy-start | bytes 19204
  7.2 91.8 %copy-start.31 = (f32[128]{0:T(128)S(1)}, f32[128]{0:T(128)}, u32[]{:S(2)}) copy-start(f32[128]{0:T(128)} %param.33) | copy-start | bytes 1540
  7.2 396.6 %all-reduce.3.cloned.1.call-start = ((), (), s32[]{:S(2)}) async-start(), calls=%async_computation | async-start | bytes 131072
  11.2 88.2 %copy-start.46 = (bf16[128,128]{1,0:T(8,128)(2,1)S(1)}, bf16[128,128]{1,0:T(8,128)(2,1)}, u32[]{:S(2)}) copy-start(bf16[128,128]{1,0:T(8,128)(2,1)} %param.34) | copy-start | bytes 98308
  11.2 88.2 %copy-start.47 = (f32[128]{0:T(128)S(1)}, f32[128]{0:T(128)}, u32[]{:S(2)}) copy-start(f32[128]{0:T(128)} %param.35) | copy-start | bytes 1540
  11.2 88.2 %copy-start.48 = (f32[128]{0:T(128)S(1)}, f32[128]{0:T(128)}, u32[]{:S(2)}) copy-start(f32[128]{0:T(128)} %param.36) | copy-start | bytes 1540
  99.6 63.5 %copy-start.37 = (f32[128]{0:T(128)}, f32[128]{0:T(128)S(1)}, u32[]{:S(2)}) copy-start(f32[128]{0:T(128)S(1)} %fusion.10) | copy-start | bytes 1540
  169.4 19.1 %copy-start.1 = (f32[32,32,128]{2,0,1:T(8,128)}, f32[32,32,128]{2,0,1:T(8,128)S(1)}, u32[]{:S(2)}) copy-start(f32[32,32,128]{2,0,1:T(8,128)S(1)} %slice_bitcast_fusion) | copy-start | bytes 1572868
  194.5 3.6 copy-start.26
  194.5 3.6 copy-start.27
  194.6 5.2 %copy-start.4 = (f32[8,4096]{1,0:T(8,128)S(1)}, f32[8,4096]{1,0:T(8,128)}, u32[]{:S(2)}) copy-start(f32[8,4096]{1,0:T(8,128)} %get-tuple-element.85) | copy-start | bytes 393220
  194.6 5.2 %copy-start.5 = (f32[8,4096]{1,0:T(8,128)S(1)}, f32[8,4096]{1,0:T(8,128)}, u32[]{:S(2)}) copy-start(f32[8,4096]{1,0:T(8,128)} %get-tuple-element.86) | copy-start | bytes 393220
  194.6 5.2 %copy-start.6 = (f32[6,4096]{1,0:T(8,128)S(1)}, f32[6,4096]{1,0:T(8,128)}, u32[]{:S(2)}) copy-start(f32[6,4096]{1,0:T(8,128)} %get-tuple-element.79) | copy-start | bytes 294916
  194.6 5.2 %copy-start.7 = (f32[6,4096]{1,0:T(8,128)S(1)}, f32[6,4096]{1,0:T(8,128)}, u32[]{:S(2)}) copy-start(f32[6,4096]{1,0:T(8,128)} %get-tuple-element.80) | copy-start | bytes 294916
  194.6 5.2 %copy-start.9 = (f32[1,4096]{1,0:T(1,128)S(1)}, f32[1,4096]{1,0:T(1,128)}, u32[]{:S(2)}) copy-start(f32[1,4096]{1,0:T(1,128)} %get-tuple-element.10) | copy-start | bytes 49156
  194.6 5.2 %copy-start.18 = (f32[1,32,128]{2,0,1:T(1,128)S(1)}, f32[1,32,128]{2,0,1:T(1,128)}, u32[]{:S(2)}) copy-start(f32[1,32,128]{2,0,1:T(1,128)} %get-tuple-element.45) | copy-start | bytes 49156
  194.6 5.2 %copy-start.19 = (f32[1,32,128]{2,0,1:T(1,128)S(1)}, f32[1,32,128]{2,0,1:T(1,128)}, u32[]{:S(2)}) copy-start(f32[1,32,128]{2,0,1:T(1,128)} %get-tuple-element.46) | copy-start | bytes 49156
  194.6 5.2 %copy-start.20 = (f32[1,32,128]{2,0,1:T(1,128)S(1)}, f32[1,32,128]{2,0,1:T(1,128)}, u32[]{:S(2)}) copy-start(f32[1,32,128]{2,0,1:T(1,128)} %get-tuple-element.47) | copy-start | bytes 49156
  194.6 5.2 %copy-start.21 = (f32[1,32,128]{2,0,1:T(1,128)S(1)}, f32[1,32,128]{2,0,1:T(1,128)}, u32[]{:S(2)}) copy-start(f32[1,32,128]{2,0,1:T(1,128)} %get-tuple-element.40) | copy-start | bytes 49156
  194.6 5.2 %copy-start.22 = (f32[1,32,128]{2,0,1:T(1,128)S(1)}, f32[1,32,128]{2,0,1:T(1,128)}, u32[]{:S(2)}) copy-start(f32[1,32,128]{2,0,1:T(1,128)} %get-tuple-element.41) | copy-start | bytes 49156
  194.7 5.2 %copy-start.23 = (f32[1,32,128]{2,0,1:T(1,128)S(1)}, f32[1,32,128]{2,0,1:T(1,128)}, u32[]{:S(2)}) copy-start(f32[1,32,128]{2,0,1:T(1,128)} %get-tuple-element.42) | copy-start | bytes 49156
  194.7 5.2 %copy-start.24 = (f32[1,32,128]{2,0,1:T(1,128)S(1)}, f32[1,32,128]{2,0,1:T(1,128)}, u32[]{:S(2)}) copy-start(f32[1,32,128]{2,0,1:T(1,128)} %get-tuple-element.43) | copy-start | bytes 49156
  194.7 5.2 %copy-start.25 = (f32[1,32,128]{2,0,1:T(1,128)S(1)}, f32[1,32,128]{2,0,1:T(1,128)}, u32[]{:S(2)}) copy-start(f32[1,32,128]{2,0,1:T(1,128)} %get-tuple-element.44) | copy-start | bytes 49156
  194.7 5.2 %copy-start.32 = (f32[48]{0:T(128)S(1)}, f32[48]{0:T(128)}, u32[]{:S(2)}) copy-start(f32[48]{0:T(128)} %get-tuple-element.111) | copy-start | bytes 580
  194.7 5.2 %copy-start.33 = (f32[48]{0:T(128)S(1)}, f32[48]{0:T(128)}, u32[]{:S(2)}) copy-start(f32[48]{0:T(128)} %get-tuple-element.112) | copy-start | bytes 580
  194.7 5.2 %copy-start.34 = (f32[48]{0:T(128)S(1)}, f32[48]{0:T(128)}, u32[]{:S(2)}) copy-start(f32[48]{0:T(128)} %get-tuple-element.113) | copy-start | bytes 580
  194.7 5.2 %copy-start.35 = (f32[48]{0:T(128)S(1)}, f32[48]{0:T(128)}, u32[]{:S(2)}) copy-start(f32[48]{0:T(128)} %get-tuple-element.114) | copy-start | bytes 580
  194.7 5.2 %copy-start.36 = (pred[48]{0:T(512)(128)(4,1)S(1)}, pred[48]{0:T(512)(128)(4,1)}, u32[]{:S(2)}) copy-start(pred[48]{0:T(512)(128)(4,1)} %fusion.98) | copy-start | bytes 148
  203.5 3.2 copy-start.29
  203.5 3.2 copy-start.30
  207.4 78.8 %copy-start.38 = (f32[128]{0:T(128)S(1)}, f32[128]{0:T(128)}, u32[]{:S(2)}) copy-start(f32[128]{0:T(128)} %copy-done.37) | copy-start | bytes 1540
  (18 other events, 48.7 us)
Sparse Core Ops, SparseCore 0:
  286.3 117.4 all-reduce.2
where the time goes:
time: 414 us; the launch traced here: 412 us
  blocking collectives  138 us (33%)
  waiting for transfers between devices  118 us (29%)
  Pallas kernels  84.4 us (20%)
  other arithmetic  44.7 us (11%)
  between operations  15.6 us (4%)
  local copies, waits for them, and re-layouts  12 us (3%)
    unnamed x2, waiting for transfers between devices  118 us
    pallas_call x1, Pallas kernels, mesh_sums(): pl.pallas_call(mesh_kernel, in_specs=[smem, smem, smem] + [vmem] * 9, out...  77.2 us
    all_gather x1, blocking collectives, local_sites(): shared = lax.all_gather(parcel, both, axis=0, tiled=False)  74.1 us
    all_gather x1, blocking collectives, local_sites(): charges = lax.all_gather(charge, both, axis=0, tiled=False)  63.4 us
  transfers between devices with their start and end apart: 1, of which 1 were waited for; matrix products, arithmetic and copies ran while one was open for 0% of the time, Pallas kernels for 0%

commit v1 on v0

--- a/solution.py
+++ b/solution.py
@@ -12,6 +12,7 @@
 LANES = 128
 CHUNK = 512
 TILE = 256
+FINE = (5, 13)
 
 highest = lax.Precision.HIGHEST
 radius_scale = 4.0
@@ -20,20 +21,160 @@
 full_turn = 2.0 * math.pi
 
 
-def charge_kernel(nearby_ref, listed_ref, scale_ref, bias_ref, mixed_ref, env_ref):
-    neigh, atoms = listed_ref.shape
+def peer_place(index, rows):
+    return (index // rows, index % rows)
+
+
+def greet_peers(me, peers, rows):
+    barrier = pltpu.get_barrier_semaphore()
+
+    def greet(k, carry):
+        pl.semaphore_signal(
+            barrier,
+            inc=1,
+            device_id=peer_place((me + k) % peers, rows),
+            device_id_type=pl.DeviceIdType.MESH,
+        )
+        return carry
+
+    lax.fori_loop(1, peers, greet, 0)
+    return barrier
+
+
+def column(table, index, length):
+    return jnp.broadcast_to(table[:length, index : index + 1], (length, LANES))
+
+
+def site_kernel(
+    position_ref,
+    neighbour_ref,
+    count_ref,
+    base_ref,
+    slope_ref,
+    scale_ref,
+    bias_ref,
+    gain_ref,
+    fit_in_ref,
+    fit_bias_ref,
+    fit_hidden_ref,
+    fit_bias_two_ref,
+    fit_out_ref,
+    sites_ref,
+    charges_ref,
+    counts_ref,
+    place_ref,
+    parcel_ref,
+    own_ref,
+    near_ref,
+    listed_ref,
+    rows_ref,
+    columns_ref,
+    gains_ref,
+    env_ref,
+    mixed_ref,
+    descriptor_ref,
+    normed_ref,
+    near_send,
+    near_recv,
+    site_send,
+    site_recv,
+    charge_send,
+    charge_recv,
+):
+    size_x = lax.axis_size("gx")
+    size_y = lax.axis_size("gy")
+    peers = size_x * size_y
+    place_x = lax.axis_index("gx")
+    place_y = lax.axis_index("gy")
+    me = place_x * size_y + place_y
+    width_x = GRID // size_x
+    width_y = GRID // size_y
+    neigh = neighbour_ref.shape[0]
+    atoms = neighbour_ref.shape[3]
+    width = scale_ref.shape[1]
+    features = gain_ref.shape[1]
+    barrier = greet_peers(me, peers, size_y)
+
+    count = count_ref[0, 0]
+    origin = (place_x * width_x + 1, place_y * width_y + 1, 1)
+    place_ref[...] = jnp.zeros_like(place_ref)
+    parcel_ref[...] = jnp.zeros_like(parcel_ref)
+    for c in range(3):
+        place_ref[c : c + 1, :] = position_ref[c, 0]
+        parcel_ref[c : c + 1, :] = (base_ref[c, 0] + origin[c]).astype(jnp.float32)
+        parcel_ref[c + 3 : c + 4, :] = slope_ref[c, 0, 0] + slope_ref[c, 3, 0] + 0.5
+    parcel_ref[6:7, :] = jnp.full((1, atoms), count, jnp.int32).astype(jnp.float32)
+    for k in range(neigh):
+        listed_ref[k : k + 1, :] = neighbour_ref[k, 0]
+
+    pl.semaphore_wait(barrier, peers - 1)
+
+    def near_copy(slot, target):
+        return pltpu.make_async_remote_copy(
+            src_ref=place_ref,
+            dst_ref=near_ref.at[slot],
+            send_sem=near_send.at[slot],
+            recv_sem=near_recv.at[slot],
+            device_id=target,
+            device_id_type=pl.DeviceIdType.MESH,
+        )
+
+    around = [(a, b) for a in (-1, 0, 1) for b in (-1, 0, 1)]
+    targets = [((place_x - a) % size_x, (place_y - b) % size_y) for a, b in around]
+    for slot in range(9):
+        if slot != 4:
+            near_copy(slot, targets[slot]).start()
+
+    def site_copy(k, place):
+        return pltpu.make_async_remote_copy(
+            src_ref=parcel_ref,
+            dst_ref=sites_ref.at[place],
+            send_sem=site_send.at[k],
+            recv_sem=site_recv.at[place],
+            device_id=peer_place((me + k) % peers, size_y),
+            device_id_type=pl.DeviceIdType.MESH,
+        )
+
+    def site_start(k, carry):
+        site_copy(k, me).start()
+        return carry
+
+    lax.fori_loop(1, peers, site_start, 0)
+    near_ref[4] = place_ref[...]
+    sites_ref[me] = parcel_ref[...]
+
+    rows_ref[...] = jnp.zeros_like(rows_ref)
+    for index, ref in enumerate((scale_ref, bias_ref)):
+        rows_ref[index : index + 1, :width] = ref[...]
+    for index, ref in enumerate((fit_bias_ref, fit_bias_two_ref, fit_out_ref)):
+        rows_ref[index + 2 : index + 3, :] = ref[...]
+    parts = -(-features // LANES)
+    for part in range(parts):
+        size = min(LANES, features - part * LANES)
+        rows_ref[part + 5 : part + 6, :size] = gain_ref[:, part * LANES : part * LANES + size]
+    columns_ref[...] = rows_ref[...].T
+    for part in range(parts):
+        size = min(LANES, features - part * LANES)
+        gains_ref[part * LANES : part * LANES + size, :] = column(columns_ref, part + 5, size)
+
+    for slot in range(9):
+        if slot != 4:
+            near_copy(slot, targets[slot]).wait_send()
+            near_copy(slot, targets[slot]).wait_recv()
+
     listed = listed_ref[...]
-    slot = listed % atoms
-    block = listed // atoms
+    slots = listed % atoms
+    blocks = listed // atoms
     square = jnp.zeros((neigh, atoms), jnp.float32)
     deltas = []
     for c in range(3):
-        center = nearby_ref[c, 4:5, :]
+        center = near_ref[4, c : c + 1, :]
         picked = jnp.zeros((neigh, atoms), jnp.float32)
-        for b in range(9):
-            row = jnp.broadcast_to(nearby_ref[c, b : b + 1, :], (neigh, atoms))
-            got = jnp.take_along_axis(row, slot, axis=1, mode="promise_in_bounds")
-            picked = jnp.where(block == b, got, picked)
+        for slot, (a, b) in enumerate(around):
+            offset = (a * width_x, b * width_y, 0)[c]
+            row = jnp.broadcast_to(near_ref[slot, c : c + 1, :] + float(offset), (neigh, atoms))
+            got = jnp.take_along_axis(row, slots, axis=1, mode="promise_in_bounds")
+            picked = jnp.where(blocks == slot, got, picked)
         delta = picked - center
         deltas.append(delta)
         square = square + delta * delta
@@ -43,162 +184,357 @@
     env_ref[0] = smooth
     for c in range(3):
         env_ref[c + 1] = deltas[c] * factor
-    mixed_ref[...] = jnp.zeros_like(mixed_ref)
-
-    def step(k, carry):
-        row = env_ref[0, pl.ds(k, 1), :]
-        embed = jnp.tanh(row * scale_ref[...] + bias_ref[...])
+
+    padded = mixed_ref.shape[1]
+    bounds = [(0, padded // 16 * 8), (padded // 16 * 8, padded)]
+    for first, last in bounds:
+        span = last - first
+        scale = jnp.broadcast_to(columns_ref[first:last, 0:1], (span, atoms))
+        shift = jnp.broadcast_to(columns_ref[first:last, 1:2], (span, atoms))
+
+        def step(k, sums):
+            rows = [env_ref[c, pl.ds(k, 1), :] for c in range(4)]
+            embed = jnp.tanh(rows[0] * scale + shift)
+            return tuple(total + embed * row for total, row in zip(sums, rows))
+
+        zero = jnp.zeros((span, atoms), jnp.float32)
+        sums = lax.fori_loop(0, neigh, step, (zero, zero, zero, zero))
         for c in range(4):
-            mixed_ref[c] += embed * env_ref[c, pl.ds(k, 1), :]
+            mixed_ref[c, first:last, :] = sums[c]
+
+    def describe(e, total):
+        value = jnp.zeros((AXIS, atoms), jnp.float32)
+        for c in range(4):
+            value = value + mixed_ref[c, pl.ds(e, 1), :] * mixed_ref[c, :AXIS, :]
+        descriptor_ref[pl.ds(pl.multiple_of(e * AXIS, AXIS), AXIS), :] = value
+        return total + value * value
+
+    total = lax.fori_loop(0, width, describe, jnp.zeros((AXIS, atoms), jnp.float32), unroll=4)
+    mean = jnp.sum(total, axis=0, keepdims=True) / features
+    scaling = lax.rsqrt(mean + norm_floor)
+    normed_ref[...] = (descriptor_ref[...] * scaling * gains_ref[...]).astype(jnp.bfloat16)
+    whole = features // LANES * LANES
+    first = jnp.dot(
+        fit_in_ref[:, :whole], normed_ref[:whole, :], preferred_element_type=jnp.float32
+    )
+    if whole < features:
+        first = first + jnp.dot(
+            fit_in_ref[:, whole:], normed_ref[whole:, :], preferred_element_type=jnp.float32
+        )
+    first = jnp.tanh(first + column(columns_ref, 2, LANES))
+    second = jnp.dot(
+        fit_hidden_ref[...], first.astype(jnp.bfloat16), preferred_element_type=jnp.float32
+    )
+    second = jnp.tanh(second + column(columns_ref, 3, LANES)) + first
+    charge = jnp.sum(column(columns_ref, 4, LANES) * second, axis=0, keepdims=True)
+    lane = lax.broadcasted_iota(jnp.int32, (1, atoms), 1)
+    own_ref[...] = jnp.where(lane < count, charge, 0.0)
+
+    def site_land(k, carry):
+        site_copy(k, me).wait_send()
+        site_copy(k, (me + k) % peers).wait_recv()
         return carry
 
-    lax.fori_loop(0, neigh, step, 0)
-
-
-def mixed_features(nearby, listed, embed_scale, embed_bias):
-    neigh, atoms = listed.shape
-    width = embed_scale.shape[0]
-    spread = jnp.broadcast_to(embed_scale[:, None], (width, atoms))
-    shift = jnp.broadcast_to(embed_bias[:, None], (width, atoms))
+    lax.fori_loop(1, peers, site_land, 0)
+
+    def charge_copy(k, place):
+        return pltpu.make_async_remote_copy(
+            src_ref=own_ref,
+            dst_ref=charges_ref.at[place],
+            send_sem=charge_send.at[k],
+            recv_sem=charge_recv.at[place],
+            device_id=peer_place((me + k) % peers, size_y),
+            device_id_type=pl.DeviceIdType.MESH,
+        )
+
+    def charge_start(k, carry):
+        charge_copy(k, me).start()
+        return carry
+
+    lax.fori_loop(1, peers, charge_start, 0)
+    charges_ref[me] = own_ref[...]
+
+    def tally(p, carry):
+        counts_ref[pl.ds(p, 1), :] = sites_ref[p, 6:7, :].astype(jnp.int32)
+        return carry
+
+    lax.fori_loop(0, peers, tally, 0)
+
+    def charge_land(k, carry):
+        charge_copy(k, me).wait_send()
+        charge_copy(k, (me + k) % peers).wait_recv()
+        return carry
+
+    lax.fori_loop(1, peers, charge_land, 0)
+
+
+def gathered_sites(collective, *args):
+    peers = lax.axis_size("gx") * lax.axis_size("gy")
+    neigh = args[1].shape[0]
+    atoms = args[1].shape[3]
+    width = args[5].shape[1]
+    features = args[7].shape[1]
+    padded = -(-width // 8) * 8
+    vmem = pl.BlockSpec(memory_space=pltpu.VMEM)
+    smem = pl.BlockSpec(memory_space=pltpu.SMEM)
+    dma = pltpu.SemaphoreType.DMA
     return pl.pallas_call(
-        charge_kernel,
-        out_shape=jax.ShapeDtypeStruct((4, width, atoms), jnp.float32),
-        scratch_shapes=[pltpu.VMEM((4, neigh, atoms), jnp.float32)],
-    )(nearby, listed, spread, shift)
-
-
-def fit_charge(mixed, count, desc_gain, fit_in, fit_bias, fit_hidden, fit_bias_two, fit_out):
-    atoms = mixed.shape[2]
-    descriptor = jnp.sum(mixed[:, :, None, :] * mixed[:, None, :AXIS, :], axis=0).reshape(-1, atoms)
-    scaling = lax.rsqrt(jnp.mean(descriptor * descriptor, axis=0) + norm_floor)
-    normed = (descriptor * scaling[None, :] * desc_gain[:, None]).astype(jnp.bfloat16)
-    first = jnp.tanh(
-        jnp.dot(fit_in, normed, preferred_element_type=jnp.float32) + fit_bias[:, None]
-    )
-    second = (
-        jnp.tanh(
-            jnp.dot(fit_hidden, first.astype(jnp.bfloat16), preferred_element_type=jnp.float32)
-            + fit_bias_two[:, None]
-        )
-        + first
-    )
-    charge = jnp.sum(fit_out[:, None] * second, axis=0)
-    slot_index = lax.broadcasted_iota(jnp.int32, (atoms,), 0)
-    return jnp.where(slot_index < count, charge, jnp.zeros((), charge.dtype))
-
-
-def pack_kernel(count_ref, sites_ref, packed_ref):
-    columns, rows, atoms = sites_ref.shape
-    packed_ref[...] = jnp.zeros_like(packed_ref)
-    lane = lax.broadcasted_iota(jnp.int32, (rows, atoms), 1)
-
-    def step(j, start):
-        count = count_ref[j]
-        tile = start // atoms
-        shift = start % atoms
-        block = jnp.where(lane < count, sites_ref[j], 0.0)
-        turned = pltpu.roll(block, shift, 1)
-        packed_ref[tile] = packed_ref[tile] + jnp.where(lane >= shift, turned, 0.0)
-        packed_ref[tile + 1] = jnp.where(lane < shift, turned, 0.0)
-        return start + count
-
-    lax.fori_loop(0, columns, step, 0)
-
-
-def pack_sites(counts, sites):
-    columns, rows, atoms = sites.shape
-    return pl.pallas_call(
-        pack_kernel,
-        in_specs=[
-            pl.BlockSpec(memory_space=pltpu.SMEM),
-            pl.BlockSpec(memory_space=pltpu.VMEM),
+        site_kernel,
+        in_specs=[vmem, vmem, smem] + [vmem] * 10,
+        out_specs=(vmem, vmem, vmem),
+        out_shape=(
+            jax.ShapeDtypeStruct((peers, 8, atoms), jnp.float32),
+            jax.ShapeDtypeStruct((peers, 1, atoms), jnp.float32),
+            jax.ShapeDtypeStruct((peers, atoms), jnp.int32),
+        ),
+        scratch_shapes=[
+            pltpu.VMEM((8, atoms), jnp.float32),
+            pltpu.VMEM((8, atoms), jnp.float32),
+            pltpu.VMEM((1, atoms), jnp.float32),
+            pltpu.VMEM((9, 8, atoms), jnp.float32),
+            pltpu.VMEM((neigh, atoms), jnp.int32),
+            pltpu.VMEM((LANES, LANES), jnp.float32),
+            pltpu.VMEM((LANES, LANES), jnp.float32),
+            pltpu.VMEM((features, atoms), jnp.float32),
+            pltpu.VMEM((4, neigh, atoms), jnp.float32),
+            pltpu.VMEM((4, padded, atoms), jnp.float32),
+            pltpu.VMEM((features, atoms), jnp.float32),
+            pltpu.VMEM((features, atoms), jnp.bfloat16),
+            dma((9,)),
+            dma((9,)),
+            dma((peers,)),
+            dma((peers,)),
+            dma((peers,)),
+            dma((peers,)),
         ],
-        out_specs=pl.BlockSpec(memory_space=pltpu.VMEM),
-        out_shape=jax.ShapeDtypeStruct((columns + 1, rows, atoms), jnp.float32),
-    )(counts, sites)
-
-
-def axis_waves(cell, start, groups):
-    def turn(index):
-        angle = ((index * cell[None, :]) % GRID).astype(jnp.float32) * (full_turn / GRID)
-        return jnp.cos(angle), jnp.sin(angle)
-
-    low_cos, low_sin = turn(jnp.arange(8, dtype=jnp.int32)[:, None])
-    high_cos, high_sin = turn(start + 8 * jnp.arange(groups, dtype=jnp.int32)[:, None])
-    low_cos, low_sin = low_cos[None], low_sin[None]
-    high_cos, high_sin = high_cos[:, None], high_sin[:, None]
-    cosine = high_cos * low_cos - high_sin * low_sin
-    sine = high_sin * low_cos + high_cos * low_sin
-    return cosine.reshape(groups * 8, -1), sine.reshape(groups * 8, -1)
-
-
-def axis_table(cosine, sine, taps, start):
-    count = cosine.shape[0]
-    angle = (start + jnp.arange(count, dtype=jnp.int32)).astype(jnp.float32) * (full_turn / GRID)
-    angle = angle[:, None]
-    real = taps[1] + (taps[0] + taps[2]) * jnp.cos(angle) + taps[3] * jnp.cos(2.0 * angle)
-    imag = (taps[2] - taps[0]) * jnp.sin(angle) + taps[3] * jnp.sin(2.0 * angle)
-    return cosine * real - sine * imag, sine * real + cosine * imag
-
-
-def plane_tables(cell, taps, slopes, start, groups):
-    cosine, sine = axis_waves(cell, start, groups)
-    parity = (1 - 2 * (cell % 2)).astype(jnp.float32)
-    zero_mode = (start + jnp.arange(groups * 8, dtype=jnp.int32) == 0)[:, None]
-    tables = []
-    for row in (taps, slopes):
-        even, odd = axis_table(cosine, sine, row, start)
-        last = parity * (row[1] + row[3] - row[0] - row[2])
-        tables.append(jnp.concatenate([even, jnp.where(zero_mode, last[None], odd)], axis=0))
-    return tables
-
-
-def plane_modes(start, count):
-    mode = start + jnp.arange(count, dtype=jnp.int32)
-    modes = jnp.concatenate([mode, jnp.where(mode == 0, GRID // 2, mode)])
-    factor = jnp.where((modes == 0) | (modes == GRID // 2), 1.0, 2.0) / GRID
-    wave = modes.astype(jnp.float32) * (full_turn / GRID)
-    return wave * wave, factor.astype(jnp.float32)
-
-
-def halves(table):
-    high = lax.reduce_precision(table, 8, 7)
-    low = table - high
-    return jnp.concatenate([high, low], axis=0).astype(jnp.bfloat16)
-
-
-def mesh_kernel(
+        compiler_params=pltpu.CompilerParams(collective_id=collective, has_side_effects=True),
+    )(*args)
+
+
+def sine(index):
+    angle = index * (full_turn / GRID)
+    square = angle * angle
+    total = jnp.full_like(square, -1.0 / 39916800.0)
+    for term in (1.0 / 362880.0, -1.0 / 5040.0, 1.0 / 120.0, -1.0 / 6.0, 1.0):
+        total = total * square + term
+    return total * angle
+
+
+def turned(index):
+    index = index - GRID * jnp.floor(index * (1.0 / GRID))
+    signed = index - GRID // 2
+    size = jnp.abs(signed)
+    near = jnp.minimum(size, GRID // 2 - size)
+    return sine(size - GRID // 4), sine(jnp.where(signed < 0, near, -near))
+
+
+def spline_taps(part):
+    rest = 1.0 - part
+    square = part * part
+    cube = square * part
+    weights = (
+        rest * rest * rest * (1.0 / 6.0),
+        (3.0 * cube - 6.0 * square + 4.0) * (1.0 / 6.0),
+        (-3.0 * cube + 3.0 * square + 3.0 * part + 1.0) * (1.0 / 6.0),
+        cube * (1.0 / 6.0),
+    )
+    slopes = (
+        -0.5 * rest * rest,
+        (3.0 * square - 4.0 * part) * 0.5,
+        (-3.0 * square + 2.0 * part + 1.0) * 0.5,
+        0.5 * square,
+    )
+    return weights, slopes
+
+
+def mode_pairs(taps, wave):
+    (cos_one, sin_one, cos_two, sin_two), (cosine, sine_part) = wave
+    real = taps[1] + (taps[0] + taps[2]) * cos_one + taps[3] * cos_two
+    imag = (taps[2] - taps[0]) * sin_one + taps[3] * sin_two
+    return cosine * real - sine_part * imag, sine_part * real + cosine * imag
+
+
+def field_kernel(
+    sites_ref,
+    charges_ref,
+    listed_ref,
+    out_ref,
     count_ref,
-    squares_ref,
-    factors_ref,
-    square_y_ref,
-    square_z_ref,
-    charge_ref,
+    packed_ref,
+    wave_ref,
+    high_ref,
     x_ref,
     slope_x_ref,
     y_ref,
     slope_y_ref,
+    lit_ref,
     z_ref,
     slope_z_ref,
-    out_ref,
+    plane_ref,
+    weight_ref,
+    row_ref,
     spectrum_ref,
     scaled_ref,
     found_ref,
+    sem,
 ):
+    size_x = lax.axis_size("gx")
+    size_y = lax.axis_size("gy")
+    columns = size_x * size_y
     modes_x = x_ref.shape[0]
     modes_y = y_ref.shape[0]
-    depth = z_ref.shape[0]
-    modes_z = depth // 2
-    columns = out_ref.shape[0]
+    modes_z = spectrum_ref.shape[1]
+    half_x = modes_x // 2
+    half_y = modes_y // 2
+    half_z = modes_z // 2
+    start_x = lax.axis_index("gx") * half_x
+    start_y = lax.axis_index("gy") * half_y
     group = 8
-    total = lax.fori_loop(0, columns, lambda j, acc: acc + count_ref[j], 0)
+    shape = (8, LANES)
+    copy = pltpu.make_async_copy(listed_ref, count_ref, sem)
+    copy.start()
+
     spectrum_ref[...] = jnp.zeros_like(spectrum_ref)
+    found_ref[...] = jnp.zeros_like(found_ref)
+    packed_ref[...] = jnp.zeros_like(packed_ref)
+    sub = lax.broadcasted_iota(jnp.int32, shape, 0).astype(jnp.float32)
+    lane = lax.broadcasted_iota(jnp.int32, shape, 1)
+    starts = [start_x.astype(jnp.float32), start_y.astype(jnp.float32), 0.0]
+    groups = [half_x // 8, half_y // 8, half_z // 8]
+    firsts = [0, groups[0], groups[0] + groups[1]]
+    for d in range(3):
+
+        def waves(g, carry):
+            mode = sub + (starts[d] + 8.0 * g.astype(jnp.float32))
+            one = turned(mode)
+            two = turned(2.0 * mode)
+            for index, value in enumerate(one + two):
+                wave_ref[firsts[d] + g, index] = value
+            return carry
+
+        lax.fori_loop(0, groups[d], waves, 0)
+
+    fine = LANES // 2
+    spot = lax.broadcasted_iota(jnp.int32, (modes_y, modes_z), 1)
+    rest = jnp.where(spot < LANES, spot, (spot - LANES) % (half_z - fine))
+    mode = jnp.where(
+        spot < LANES, FINE[0] * 8 + spot % fine, jnp.where(rest < FINE[0] * 8, rest, rest + fine)
+    ).astype(jnp.float32)
+    factor = jnp.where(mode == 0, 1.0, 2.0) * (1.0 / GRID)
+    wave = mode * (full_turn / GRID)
+    square = wave * wave
+    spot = lax.broadcasted_iota(jnp.int32, (modes_y, modes_z), 0)
+    mode = start_y + jnp.where(spot < half_y, spot, spot - half_y)
+    mode = jnp.where((mode == 0) & (spot >= half_y), GRID // 2, mode)
+    ends = (mode == 0) | (mode == GRID // 2)
+    factor = factor * jnp.where(ends, 1.0, 2.0) * (1.0 / GRID)
+    wave = mode.astype(jnp.float32) * (full_turn / GRID)
+    square = square + wave * wave
+    decay = -0.5 * screen_width * screen_width
+    plane_ref[...] = square
+    weight_ref[...] = jnp.exp(square * decay) * factor * (2.0 * full_turn)
+    spot = lax.broadcasted_iota(jnp.int32, (modes_x, LANES), 0)
+    mode = start_x + jnp.where(spot < half_x, spot, spot - half_x)
+    mode = jnp.where((mode == 0) & (spot >= half_x), GRID // 2, mode)
+    ends = (mode == 0) | (mode == GRID // 2)
+    wave = mode.astype(jnp.float32) * (full_turn / GRID)
+    square = wave * wave
+    row_ref[0] = square
+    row_ref[1] = jnp.exp(square * decay) * jnp.where(ends, 1.0, 2.0) * (1.0 / GRID)
+
+    copy.wait()
+
+    def pack(j, start):
+        count = count_ref[j, 0]
+        tile = start // LANES
+        shift = start % LANES
+        site = jnp.where(
+            lax.broadcasted_iota(jnp.int32, shape, 0) == 7,
+            jnp.broadcast_to(charges_ref[j], shape),
+            sites_ref[j],
+        )
+        turn = pltpu.roll(jnp.where(lane < count, site, 0.0), shift, 1)
+        packed_ref[tile] = packed_ref[tile] + jnp.where(lane >= shift, turn, 0.0)
+        packed_ref[tile + 1] = jnp.where(lane < shift, turn, 0.0)
+        return start + count
+
+    total = lax.fori_loop(0, columns, pack, 0)
+    chunks = (total + CHUNK - 1) // CHUNK
+    order = list(range(*FINE)) + list(range(FINE[0])) + list(range(FINE[1], groups[2]))
+
+    def tables(tile, carry):
+        lanes = pl.ds(pl.multiple_of(tile * LANES, LANES), LANES)
+        charge = jnp.broadcast_to(packed_ref[tile, 7:8, :], shape)
+        for d in range(3):
+            cell = jnp.broadcast_to(packed_ref[tile, d : d + 1, :], shape)
+            part = jnp.broadcast_to(packed_ref[tile, d + 3 : d + 4, :], shape)
+            weights, slopes = spline_taps(part)
+            low_cos, low_sin = turned(sub * cell)
+            for h in range(-(-groups[d] // 8)):
+                high_cos, high_sin = turned((starts[d] + 8.0 * (sub + 8.0 * h)) * cell)
+                high_ref[0, 8 * h : 8 * h + 8] = high_cos
+                high_ref[1, 8 * h : 8 * h + 8] = high_sin
+
+            def pairs(g):
+                high_cos = high_ref[0, g : g + 1]
+                high_sin = high_ref[1, g : g + 1]
+                constants = tuple(wave_ref[firsts[d] + g, index] for index in range(4))
+                wave = (
+                    constants,
+                    (
+                        high_cos * low_cos - high_sin * low_sin,
+                        high_sin * low_cos + high_cos * low_sin,
+                    ),
+                )
+                return mode_pairs(weights, wave) + mode_pairs(slopes, wave)
+
+            if d < 2:
+                half = groups[d] * 8
+                for g in range(groups[d]):
+                    even, odd, slope_even, slope_odd = pairs(g)
+                    if g == 0:
+                        parity = cell - 2.0 * jnp.floor(cell * 0.5)
+                        parity = 1.0 - 2.0 * parity
+                        first = (sub + starts[d]) == 0
+                        last = parity * (weights[1] + weights[3] - weights[0] - weights[2])
+                        odd = jnp.where(first, last, odd)
+                        last = parity * (slopes[1] + slopes[3] - slopes[0] - slopes[2])
+                        slope_odd = jnp.where(first, last, slope_odd)
+                    table = (x_ref, y_ref)[d]
+                    slope = (slope_x_ref, slope_y_ref)[d]
+                    table[8 * g : 8 * g + 8, lanes] = even
+                    table[half + 8 * g : half + 8 * g + 8, lanes] = odd
+                    slope[8 * g : 8 * g + 8, lanes] = slope_even
+                    slope[half + 8 * g : half + 8 * g + 8, lanes] = slope_odd
+                    if d == 1:
+                        lit_ref[8 * g : 8 * g + 8, lanes] = even * charge
+                        lit_ref[half + 8 * g : half + 8 * g + 8, lanes] = odd * charge
+                continue
+            for index in range(0, len(order), 2):
+                both = [pairs(order[index]), pairs(order[index + 1])]
+                fine_part = index < FINE[1] - FINE[0]
+                if fine_part:
+                    spots = (8 * index, fine + 8 * index)
+                else:
+                    spots = (LANES + 8 * index - fine, half_z + 8 * index)
+                for which in range(4):
+                    table = z_ref if which < 2 else slope_z_ref
+                    value = jnp.concatenate([both[0][which], both[1][which]], axis=0)
+                    high = value.astype(jnp.bfloat16)
+                    row = spots[which % 2]
+                    table[row : row + 16, lanes] = high
+                    if fine_part:
+                        low = value - high.astype(jnp.float32)
+                        row = row + modes_z
+                        table[row : row + 16, lanes] = low.astype(jnp.bfloat16)
+        return carry
+
+    lax.fori_loop(0, chunks * (CHUNK // LANES), tables, 0)
 
     def gather_chunk(chunk, carry):
         lanes = pl.ds(pl.multiple_of(chunk * CHUNK, CHUNK), CHUNK)
-        y = y_ref[:, lanes] * charge_ref[:, lanes]
-        high = z_ref[:modes_z, lanes]
-        low = z_ref[modes_z:, lanes]
+        y = lit_ref[:, lanes]
+        z = z_ref[:, lanes]
 
         def rows(g, inner):
             x = x_ref[pl.ds(pl.multiple_of(g * group, group), group), lanes]
@@ -207,35 +543,30 @@
             )
             where = pl.ds(pl.multiple_of(g * group * modes_y, group * modes_y), group * modes_y)
             form = (((1,), (1,)), ((), ()))
-            spectrum_ref[where, :] += lax.dot_general(
-                left, high, form, preferred_element_type=jnp.float32
-            ) + lax.dot_general(left, low, form, preferred_element_type=jnp.float32)
+            both = lax.dot_general(left, z, form, preferred_element_type=jnp.float32)
+            spectrum_ref[where, :LANES] += both[:, :LANES] + both[:, modes_z:]
+            spectrum_ref[where, LANES:] += both[:, LANES:modes_z]
             return inner
 
         return lax.fori_loop(0, modes_x // group, rows, carry)
 
-    lax.fori_loop(0, (total + CHUNK - 1) // CHUNK, gather_chunk, 0)
-
-    square_y = square_y_ref[:, 0:1]
-    factor_y = square_y_ref[:, 1:2]
-    square_z = square_z_ref[0:1, :]
-    factor_z = square_z_ref[1:2, :]
-    plane = square_y + square_z
-    weight = factor_y * factor_z * (2.0 * full_turn)
+    lax.fori_loop(0, chunks, gather_chunk, 0)
 
     def scale(a, carry):
-        square = plane + squares_ref[a]
+        def spread(ref, width):
+            row = ref[pl.ds(a, 1), :]
+            return jnp.concatenate([row] * (width // LANES), axis=1)
+
+        square = plane_ref[...] + spread(row_ref.at[0], modes_z)
         safe = jnp.where(square > 0, square, 1.0)
-        green = jnp.exp(square * (-0.5 * screen_width * screen_width)) / safe
-        green = jnp.where(square > 0, green, 0.0) * (weight * factors_ref[a])
+        green = jnp.where(square > 0, weight_ref[...], 0.0) / safe * spread(row_ref.at[1], modes_z)
         where = pl.ds(pl.multiple_of(a * modes_y, modes_y), modes_y)
         value = (spectrum_ref[where, :] * green).astype(jnp.bfloat16)
         scaled_ref[where, :modes_z] = value
-        scaled_ref[where, modes_z:] = value
+        scaled_ref[where, modes_z:] = value[:, :LANES]
         return carry
 
     lax.fori_loop(0, modes_x, scale, 0)
-    found_ref[...] = jnp.zeros_like(found_ref)
 
     def tile_step(tile, carry):
         lanes = pl.ds(pl.multiple_of(tile * TILE, TILE), TILE)
@@ -276,7 +607,6 @@
         return carry
 
     lax.fori_loop(0, (total + TILE - 1) // TILE, tile_step, 0)
-    lane = lax.broadcasted_iota(jnp.int32, (8, LANES), 1)
 
     def place(j, start):
         tile = start // LANES
@@ -284,31 +614,102 @@
         back = (LANES - shift) % LANES
         first = pltpu.roll(found_ref[tile], back, 1)
         second = pltpu.roll(found_ref[tile + 1], back, 1)
-        out_ref[j] = jnp.where(lane < LANES - shift, first, second)
-        return start + count_ref[j]
+        out_ref[j] = jnp.where(lane < LANES - shift, first, second)[:4]
+        return start + count_ref[j, 0]
 
     lax.fori_loop(0, columns, place, 0)
 
 
-def mesh_sums(counts, squares_x, factors_x, side_y, side_z, charge, tables):
-    columns = counts.shape[0]
-    modes_x = tables[0].shape[0]
-    modes_y = tables[2].shape[0]
-    modes_z = tables[4].shape[0] // 2
+def mesh_sums(sites, charges, counts):
+    size_x = lax.axis_size("gx")
+    size_y = lax.axis_size("gy")
+    columns, _, atoms = sites.shape
+    slots = -(-(columns * atoms) // CHUNK) * CHUNK
+    modes_x = GRID // size_x
+    modes_y = GRID // size_y
+    groups = (modes_x + modes_y + GRID) // 16
     vmem = pl.BlockSpec(memory_space=pltpu.VMEM)
-    smem = pl.BlockSpec(memory_space=pltpu.SMEM)
+    table = lambda rows: pltpu.VMEM((rows, slots), jnp.float32)
     return pl.pallas_call(
-        mesh_kernel,
-        in_specs=[smem, smem, smem] + [vmem] * 9,
+        field_kernel,
+        in_specs=[vmem, vmem, vmem],
         out_specs=vmem,
-        out_shape=jax.ShapeDtypeStruct((columns, 8, LANES), jnp.float32),
+        out_shape=jax.ShapeDtypeStruct((columns, 4, atoms), jnp.float32),
         scratch_shapes=[
-            pltpu.VMEM((modes_x * modes_y, modes_z), jnp.float32),
-            pltpu.VMEM((modes_x * modes_y, 2 * modes_z), jnp.bfloat16),
-            pltpu.VMEM((tables[0].shape[1] // LANES + 2, 8, LANES), jnp.float32),
+            pltpu.SMEM(counts.shape, jnp.int32),
+            pltpu.VMEM((slots // LANES + 2, 8, LANES), jnp.float32),
+            pltpu.VMEM((groups, 4, 8, LANES), jnp.float32),
+            pltpu.VMEM((2, 24, LANES), jnp.float32),
+            table(modes_x),
+            table(modes_x),
+            table(modes_y),
+            table(modes_y),
+            table(modes_y),
+            pltpu.VMEM((GRID + LANES, slots), jnp.bfloat16),
+            pltpu.VMEM((GRID + LANES, slots), jnp.bfloat16),
+            pltpu.VMEM((modes_y, GRID), jnp.float32),
+            pltpu.VMEM((modes_y, GRID), jnp.float32),
+            pltpu.VMEM((2, modes_x, LANES), jnp.float32),
+            pltpu.VMEM((modes_x * modes_y, GRID), jnp.float32),
+            pltpu.VMEM((modes_x * modes_y, GRID + LANES), jnp.bfloat16),
+            pltpu.VMEM((slots // LANES + 2, 8, LANES), jnp.float32),
+            pltpu.SemaphoreType.DMA,
         ],
         compiler_params=pltpu.CompilerParams(vmem_limit_bytes=60 * 2**20),
-    )(counts, squares_x, factors_x, side_y, side_z, charge, *tables)
+    )(sites, charges, counts)
+
+
+def finish_kernel(sums_ref, charge_ref, out_ref, landed_ref, send_sem, recv_sem):
+    rows = lax.axis_size("gy")
+    peers = lax.axis_size("gx") * rows
+    me = lax.axis_index("gx") * rows + lax.axis_index("gy")
+    pl.semaphore_wait(greet_peers(me, peers, rows), peers - 1)
+
+    def copy_to(k, place):
+        peer = (me + k) % peers
+        return pltpu.make_async_remote_copy(
+            src_ref=sums_ref.at[peer],
+            dst_ref=landed_ref.at[place],
+            send_sem=send_sem.at[k],
+            recv_sem=recv_sem.at[place],
+            device_id=peer_place(peer, rows),
+            device_id_type=pl.DeviceIdType.MESH,
+        )
+
+    def send(k, carry):
+        copy_to(k, me).start()
+        return carry
+
+    lax.fori_loop(1, peers, send, 0)
+    landed_ref[me] = sums_ref[me]
+
+    def land(k, carry):
+        copy_to(k, me).wait_send()
+        copy_to(k, (me + k) % peers).wait_recv()
+        return carry
+
+    lax.fori_loop(1, peers, land, 0)
+    total = jnp.sum(landed_ref[...], axis=0)
+    charge = charge_ref[me]
+    out_ref[0:1] = 0.5 * charge * total[0:1]
+    out_ref[1:4] = -charge * total[1:4]
+
+
+def finish(sums, charge, collective):
+    peers, rows, atoms = sums.shape
+    vmem = pl.BlockSpec(memory_space=pltpu.VMEM)
+    return pl.pallas_call(
+        finish_kernel,
+        out_shape=jax.ShapeDtypeStruct((4, atoms), jnp.float32),
+        in_specs=[vmem, vmem],
+        out_specs=vmem,
+        scratch_shapes=[
+            pltpu.VMEM((peers, rows, atoms), jnp.float32),
+            pltpu.SemaphoreType.DMA((peers,)),
+            pltpu.SemaphoreType.DMA((peers,)),
+        ],
+        compiler_params=pltpu.CompilerParams(collective_id=collective, has_side_effects=True),
+    )(sums, charge)
 
 
 def local_sites(
@@ -327,85 +728,26 @@
     fit_bias_two,
     fit_out,
 ):
-    both = ("gx", "gy")
-    columns_x = lax.axis_size("gx")
-    columns_y = lax.axis_size("gy")
-    columns = columns_x * columns_y
-    place_x = lax.axis_index("gx")
-    place_y = lax.axis_index("gy")
-    width_x = GRID // columns_x
-    width_y = GRID // columns_y
     atoms = positions.shape[3]
-    origin = jnp.stack([place_x * width_x, place_y * width_y, 0])
-    cells = (stencil_base[:, 0, 0, :] + origin[:, None] + 1).astype(jnp.float32)
-    counted = jnp.broadcast_to(live_count.astype(jnp.float32), (1, atoms))
-    parcel = jnp.concatenate(
-        [
-            positions[:, 0, 0, :],
-            counted,
-            cells,
-            spline_weight[:, :, 0, 0, :].reshape(12, atoms),
-            spline_slope[:, :, 0, 0, :].reshape(12, atoms),
-        ],
-        axis=0,
-    )
-    shared = lax.all_gather(parcel, both, axis=0, tiled=False)
-    counts = shared[:, 3, 0].astype(jnp.int32)
-    near = []
-    for stride_x in (-1, 0, 1):
-        for stride_y in (-1, 0, 1):
-            other_x = (place_x + stride_x) % columns_x
-            other_y = (place_y + stride_y) % columns_y
-            block = lax.dynamic_index_in_dim(
-                shared, other_x * columns_y + other_y, axis=0, keepdims=False
-            )[:3]
-            offset = jnp.array([stride_x * width_x, stride_y * width_y, 0], jnp.float32)
-            near.append(block + offset[:, None])
-    mixed = mixed_features(
-        jnp.stack(near, axis=1), neighbours[:, 0, 0, :], embed_scale, embed_bias
-    )
-    charge = fit_charge(
-        mixed, live_count[0, 0], desc_gain, fit_in, fit_bias, fit_hidden, fit_bias_two, fit_out
-    )
-    charges = lax.all_gather(charge, both, axis=0, tiled=False)
-    sites = jnp.concatenate(
-        [shared[:, 4:], charges[:, None, :], jnp.zeros((columns, 4, atoms), jnp.float32)], axis=1
-    )
-    packed = pack_sites(counts, sites)[:columns]
-    slots = -(-(columns * atoms) // CHUNK) * CHUNK
-    packed = jnp.transpose(packed, (1, 0, 2)).reshape(packed.shape[1], columns * atoms)
-    packed = jnp.pad(packed, ((0, 0), (0, slots - columns * atoms)))
-    cells = packed[:3].astype(jnp.int32)
-    taps = packed[3:15].reshape(3, 4, -1)
-    slopes = packed[15:27].reshape(3, 4, -1)
-    half_x = GRID // columns_x // 2
-    half_y = GRID // columns_y // 2
-    start_x = place_x * half_x
-    start_y = place_y * half_y
-    table_x, slope_x = plane_tables(cells[0], taps[0], slopes[0], start_x, half_x // 8)
-    table_y, slope_y = plane_tables(cells[1], taps[1], slopes[1], start_y, half_y // 8)
-    cosine, sine = axis_waves(cells[2], 0, GRID // 16)
-    table_z = halves(jnp.concatenate(axis_table(cosine, sine, taps[2], 0), axis=0))
-    slope_z = halves(jnp.concatenate(axis_table(cosine, sine, slopes[2], 0), axis=0))
-    squares_x, factors_x = plane_modes(start_x, half_x)
-    squares_y, factors_y = plane_modes(start_y, half_y)
-    mode_z = jnp.arange(GRID, dtype=jnp.int32) % (GRID // 2)
-    wave_z = mode_z.astype(jnp.float32) * (full_turn / GRID)
-    factors_z = jnp.where(mode_z == 0, 1.0, 2.0).astype(jnp.float32) / GRID
-    side_y = jnp.stack([squares_y, factors_y], axis=1)
-    side_z = jnp.stack([wave_z * wave_z, factors_z], axis=0)
-    sums = mesh_sums(
-        counts,
-        squares_x,
-        factors_x,
-        side_y,
-        side_z,
-        packed[27:28],
-        (table_x, slope_x, table_y, slope_y, table_z, slope_z),
-    )
-    mine = lax.psum_scatter(sums[:, :4], both, scatter_dimension=0, tiled=True)[0]
-    energy = (0.5 * charge * mine[0]).reshape(1, 1, atoms)
-    force = (-charge[None, :] * mine[1:]).reshape(3, 1, 1, atoms)
+    sites, charges, counts = gathered_sites(
+        1,
+        positions,
+        neighbours,
+        live_count,
+        stencil_base,
+        spline_slope,
+        embed_scale[None, :],
+        embed_bias[None, :],
+        desc_gain[None, :],
+        fit_in,
+        fit_bias[None, :],
+        fit_hidden,
+        fit_bias_two[None, :],
+        fit_out[None, :],
+    )
+    mine = finish(mesh_sums(sites, charges, counts), charges, 2)
+    energy = mine[0].reshape(1, 1, atoms)
+    force = mine[1:].reshape(3, 1, 1, atoms)
     return (energy, force)
 
 

time: 414 us -> 92.1 us (0.22)
  blocking collectives: 138 us -> 0 us
  waiting for transfers between devices: 118 us -> 0 us
  other arithmetic: 44.7 us -> 0 us
  between operations: 15.6 us -> 1.32 us
  local copies, waits for them, and re-layouts: 12 us -> 5.04 us
    all_gather x2 -> x0, blocking collectives: 138 us -> none  [the longest x1 74.1 us: local_sites(): shared = lax.all_gather(parcel, both, axis=0, tiled=False)]
    unnamed x2 -> x0, waiting for transfers between devices: 118 us -> none
    concatenate x8 -> x0, other arithmetic: 12.3 us -> none  [the longest x2 6.91 us: halves(): return jnp.concatenate([high, low], axis=0).astype(jnp.bfloat16)]
    cos x6 -> x0, other arithmetic: 7.2 us -> none  [turn(): return (jnp.cos(angle), jnp.sin(angle))]
    sub x3 -> x0, other arithmetic: 5.18 us -> none  [axis_table(): return (cosine * real - sine * imag, sine * real + cosine * imag)]
  transfers between devices with their start and end apart: 1 -> 0, of which waited for: 1 -> 0; matrix products, arithmetic and copies ran while one was open for 0% -> 0% of each run, Pallas kernels for 0% -> 0%
where the time goes in v1:
time: 92.1 us; the launch traced here: 91.8 us
  Pallas kernels  85.4 us (93%)
  local copies, waits for them, and re-layouts  5.04 us (5%)
  between operations  1.32 us (1%)
    pallas_call x1, Pallas kernels, mesh_sums(): pl.pallas_call(field_kernel, in_specs=[vmem, vmem, vmem], out_specs=vmem,...  54.3 us
    pallas_call x1, Pallas kernels, gathered_sites(): pl.pallas_call(site_kernel, in_specs=[vmem, vmem, smem] + [vmem] * 10, ou...  21.5 us
    pallas_call x1, Pallas kernels, finish(): pl.pallas_call(finish_kernel, out_shape=jax.ShapeDtypeStruct((4, atoms),...  9.66 us
    unnamed x4, local copies, waits for them, and re-layouts  2.56 us

profile of v1, /device:TPU:0, one launch (start us, length us, event | category | flops | bytes accessed | tf_op | source)
XLA Modules:
  0.0 91.8 jit_solution(15294770374188755541)
XLA Ops:
  0.6 0.0 copy-start
  1.3 0.0 copy-done
  1.3 0.6 broadcast_in_dim.20.gain_ref
  1.9 2.0 %copy.15.fit_in_ref = bf16[128,1600]{1,0:T(8,128)(2,1)} copy(bf16[128,1600]{0,1:T(8,128)(2,1)} %param.22) | data formatting | bytes 819200 | tf_op args[9]
  3.9 21.5 %shard_map.140 = (f32[32,8,128]{2,1,0:T(8,128)}, f32[32,1,128]{2,1,0:T(1,128)}, s32[32,128]{1,0:T(8,128)}) custom-call(f32[3,1,1,128]{3,2,1,0:T(1,128)} %position_ref.1, s32[32,1,1,128]{3,2,1,0:T(1,128)} %neighbour_ref.1, s32[1,1]{1,0:T(1,128)S(6)} %copy.17.count_ref, s32[3,1,1,128]{3,2,1,0:T(1,128)} %base_ref.1, f32[3,4,1,1,128]{4,3,2,1,0:T(1,128)} %slope_ref.1, ...), custom_call_target="tpu_custom_call" | custom-call | tf_op jit(solution)/shard_map/pallas_call | solution.py:281
  25.4 54.3 %shard_map.141.sums_ref = f32[32,4,128]{2,1,0:T(4,128)} custom-call(f32[32,8,128]{2,1,0:T(8,128)} %get-tuple-element.5.sites_ref, f32[32,1,128]{2,1,0:T(1,128)} %get-tuple-element.6.charges_ref.charge_ref, s32[32,128]{1,0:T(8,128)} %get-tuple-element.7.listed_ref), custom_call_target="tpu_custom_call" | custom-call | tf_op jit(solution)/shard_map/pallas_call | solution.py:633
  79.7 9.7 %shard_map.142 = f32[4,128]{1,0:T(4,128)} custom-call(f32[32,4,128]{2,1,0:T(4,128)} %shard_map.141.sums_ref, f32[32,1,128]{2,1,0:T(1,128)} %get-tuple-element.6.charges_ref.charge_ref), custom_call_target="tpu_custom_call" | custom-call | tf_op jit(solution)/shard_map/pallas_call | solution.py:701
  89.3 1.2 %slice_bitcast_fusion.1 = f32[1,1,128]{2,1,0:T(1,128)} fusion(f32[4,128]{1,0:T(4,128)} %shard_map.142), kind=kLoop, calls=%fused_computation.1 | loop fusion | bytes 1024 | tf_op jit(solution)/shard_map/reshape;squeeze | solution.py:749
  90.5 0.7 slice_bitcast_fusion
  91.2 0.6 copy.16
Async XLA Ops:
  0.6 0.7 copy-start
